TPU v7x, 256 devices: a whole 4x4x8 slice. The times are simulated.
256 devices in a mesh: replica: 16 (over z_hi, x), shard: 16 (over y, z_lo, core).
Axes of the slice: x: 4, y: 4, z: 8 (z_hi: 4, z_lo: 2; z = z_hi * 2 + z_lo), core: 2. Of those that a mesh axis runs over, the one named last changes fastest.
Arguments:
- deltas: bfloat16 [16, 8192, 8192], P('replica', 'shard')
- master: float32 [8192, 8192], P('shard', 'replica'), may hold values from -6 to 6
- momentum: float32 [8192, 8192], P('shard', 'replica'), may hold values from -6 to 6
- block_owner: int32 [32, 1], replicated, may hold values from 0 to 15; in each aligned block of 32 rows (0 to 31, 32 to 63, ...) at most 4 rows name the same one
Outputs:
- master_out: float32 [8192, 8192], P('shard', 'replica')
- momentum_out: float32 [8192, 8192], P('shard', 'replica')
- params: bfloat16 [4096, 8192], P(None, 'replica')
Inputs may be any that keep to these rules, and one draw needn't show every extreme that they name: `block_owner`: every shard owns at least one block and at most 4; some shard owns exactly 4. Rows of slots that are not live hold arbitrary deltas.
All inputs are finite; a program needn't handle non-finite values.
Results may differ from a plain program's by a relative error of at most 0.01.
Values may be sent and summed in bfloat16 or wider, within the bound.
A program may use at most 128 MiB of HBM per device.

v0:
```python
import functools

import jax
import jax.numpy as jnp
from jax import lax
from jax.sharding import Mesh
from jax.sharding import PartitionSpec as P

BLOCK_ROWS = 128
SLOTS = 4
REPLICA = ("replica_0", "replica_1")
SHARD = ("shard_0", "shard_1", "shard_2")
REPLICA_SHARD = ("replica_0", "replica_1", "shard_0", "shard_1", "shard_2")


def over_axes(x, axes):
    return functools.reduce(lax.psum, axes, x)


def on_device(deltas, master, momentum, block_owner):
    replicas = lax.axis_size(REPLICA)
    me_shard = lax.axis_index(SHARD)
    width = deltas.shape[2]
    cols = master.shape[1]
    owner = block_owner[:, 0]
    blocks = owner.shape[0]
    mine_count = jnp.sum((owner == me_shard).astype(jnp.int32))
    live = jnp.arange(SLOTS, dtype=jnp.int32) < mine_count
    live_rows = jnp.repeat(live, BLOCK_ROWS)[:, None]
    local = jnp.where(live_rows, deltas[0].astype(jnp.float32), jnp.float32(0.0))
    mine = lax.psum_scatter(
        local.astype(jnp.bfloat16), REPLICA, scatter_dimension=1, tiled=True
    ).astype(jnp.float32)
    avg = mine / replicas
    total = over_axes(jnp.sum(avg * avg), REPLICA_SHARD)
    limit = 0.5 * jnp.sqrt(jnp.float32(blocks * BLOCK_ROWS * width))
    factor = jnp.minimum(jnp.float32(1.0), limit / (jnp.sqrt(total) + 1e-06))
    grad = factor * avg
    momentum_out = jnp.where(live_rows, 0.9 * momentum + grad, momentum)
    master_out = jnp.where(live_rows, master - 0.7 * (grad + 0.9 * momentum_out), master)
    updated = master_out.astype(jnp.bfloat16).reshape(SLOTS, BLOCK_ROWS, cols)
    index = jnp.arange(blocks, dtype=jnp.int32)
    same = (owner[None, :] == owner[:, None]) & (index[None, :] < index[:, None])
    before = jnp.sum(same.astype(jnp.int32), axis=1)
    flat = owner * SLOTS + before
    piece = lax.all_gather(updated, SHARD, axis=0, tiled=True)
    count = piece.shape[0]
    positions = jnp.arange(count, dtype=jnp.int32)
    picker = (flat[:, None] == positions[None, :]).astype(jnp.bfloat16)
    placed = jnp.einsum("bj,jrc->brc", picker, piece, preferred_element_type=jnp.float32)
    params = placed.astype(jnp.bfloat16).reshape(blocks * BLOCK_ROWS, cols)
    return (master_out, momentum_out, params)


def solution(mesh):
    finer = Mesh(
        mesh.devices.reshape(4, 4, 4, 2, 2),
        ("replica_0", "replica_1", "shard_0", "shard_1", "shard_2"),
    )
    in_specs = (P(REPLICA, SHARD, None), P(SHARD, REPLICA), P(SHARD, REPLICA), P())
    out_specs = (P(SHARD, REPLICA), P(SHARD, REPLICA), P(None, REPLICA))
    return jax.shard_map(
        on_device, mesh=finer, in_specs=in_specs, out_specs=out_specs, check_vma=False
    )
```

profile of v0, /device:TPU:1, one launch (start us, length us, event | category | flops | bytes accessed | tf_op | source)
XLA Modules:
  0.0 265.7 jit_solution(12829771742739522074)
XLA Ops:
  7.2 0.0 reduce-scatter.2.cloned.1.call-start
  7.2 1.3 fusion.16
  8.5 0.6 iota_compare_fusion.2
  9.2 0.1 broadcast_bitcast_fusion
  9.2 10.1 %fusion = bf16[512,8192]{1,0:T(8,128)(2,1)} fusion(bf16[1,512,8192]{2,1,0:T(8,128)(2,1)} %param.4, pred[512]{0:T(512)(128)(4,1)S(1)} %broadcast_bitcast_fusion), kind=kLoop, calls=%fused_computation.1 | loop fusion | flops 12582912 | bytes 16777728 | tf_op jit(solution)/shard_map/convert_element_type | solution.py:32
  19.4 0.0 copy-start
  19.4 0.0 copy-start.1
  19.4 0.0 copy-start.2
  19.4 0.0 reduce-scatter.2.cloned.1.call-update
  19.4 0.0 all-gather.2.cloned.1.call-start
  19.5 123.2 %reduce-scatter.2.cloned.1.call-done = bf16[512,512]{1,0:T(8,128)(2,1)} async-done(((bf16[512,8192]{1,0:T(8,128)(2,1)}), bf16[512,512]{1,0:T(8,128)(2,1)}) %reduce-scatter.2.cloned.1.call-update) | async-done | bytes 524304 | tf_op jit(solution)/shard_map/reduce_scatter | solution.py:31
  142.6 1.9 fusion.11
  144.6 9.7 %psum.35 = f32[]{:T(128)} all-reduce(f32[]{:T(128)} %fusion.11), channel_id=1, replica_groups=mesh['replica_0'=4,'replica_1'=4,'shard_0'=4,'shard_1'=2,'shard_2'=2] {'..., use_global_device_ids=true, to_apply=%region_3.4 | all-reduce | flops 1 | bytes 8 | tf_op jit(solution)/shard_map/psum | solution.py:17
  154.3 8.6 %psum.36 = f32[]{:T(128)} all-reduce(f32[]{:T(128)} %psum.35), channel_id=1, replica_groups=mesh['replica_0'=4,'replica_1'=4,'shard_0'=4,'shard_1'=2,'shard_2'=2] {'..., use_global_device_ids=true, to_apply=%region_4.5 | all-reduce | flops 1 | bytes 8 | tf_op jit(solution)/shard_map/psum | solution.py:17
  162.9 9.1 %psum.37 = f32[]{:T(128)} all-reduce(f32[]{:T(128)} %psum.36), channel_id=1, replica_groups=mesh['replica_0'=4,'replica_1'=4,'shard_0'=4,'shard_1'=2,'shard_2'=2] {'..., use_global_device_ids=true, to_apply=%region_5.6 | all-reduce | flops 1 | bytes 8 | tf_op jit(solution)/shard_map/psum | solution.py:17
  171.9 4.6 %psum.38 = f32[]{:T(128)} all-reduce(f32[]{:T(128)} %psum.37), channel_id=1, replica_groups=mesh['replica_0'=4,'replica_1'=4,'shard_0'=4,'shard_1'=2,'shard_2'=2] {'..., use_global_device_ids=true, to_apply=%region_6.7 | all-reduce | flops 1 | bytes 8 | tf_op jit(solution)/shard_map/psum | solution.py:17
  176.5 11.7 %psum.39 = f32[]{:T(128)} all-reduce(f32[]{:T(128)} %psum.38), channel_id=1, replica_groups=mesh['replica_0'=4,'replica_1'=4,'shard_0'=4,'shard_1'=2,'shard_2'=2] {'..., use_global_device_ids=true, to_apply=%region_7.8 | all-reduce | flops 1 | bytes 8 | tf_op jit(solution)/shard_map/psum | solution.py:17
  189.0 0.0 copy-done
  189.0 0.0 copy-done.1
  189.0 2.9 %fusion.18 = (bf16[512,512]{1,0:T(8,128)(2,1)}, f32[512,512]{1,0:T(8,128)}, f32[512,512]{1,0:T(8,128)}) fusion(f32[512,512]{1,0:T(8,128)S(1)} %copy-done, f32[]{:T(128)S(6)} %mul.39, bf16[512,512]{1,0:T(8,128)(2,1)} %reduce-scatter.2.cloned.1.call-done, pred[512]{0:T(512)(128)(4,1)S(1)} %broadcast_bitcast_fusion, f32[512,512]{1,0:T(8,128)S(1)} %copy-done.1), kind=kLoop, calls=%fused_computation.26 | loop fusion | flops 2883584 | bytes 5243396 | tf_op jit(solution)/shard_map/convert_element_type | solution.py:41
  191.9 0.0 all-gather.2.cloned.1.call-update
  191.9 0.0 copy-done.2
  191.9 0.2 convert_reduce_fusion
  192.1 49.0 %all-gather.2.cloned.1.call-done = bf16[64,128,512]{2,1,0:T(8,128)(2,1)} async-done(((bf16[4,128,512]{2,1,0:T(8,128)(2,1)}), bf16[64,128,512]{2,1,0:T(8,128)(2,1)}) %all-gather.2.cloned.1.call-update) | async-done | bytes 8388624 | tf_op jit(solution)/shard_map/all_gather | solution.py:46
  241.1 13.4 %fusion.3 = bf16[32,128,512]{2,0,1:T(8,128)(2,1)S(1)} fusion(bf16[64,128,512]{2,1,0:T(8,128)(2,1)} %all-gather.2.cloned.1.call-done, s32[32]{0:T(128)S(1)} %fusion.17), kind=kOutput, calls=%fused_computation.4 | convolution fusion | flops 270534656 | bytes 12583040 | tf_op jit(solution)/shard_map/bj,jrc->brc/dot_general | solution.py:50
  254.5 4.4 %copy.12 = bf16[32,128,512]{2,1,0:T(8,128)(2,1)} copy(bf16[32,128,512]{2,0,1:T(8,128)(2,1)S(1)} %fusion.3) | data formatting | bytes 8388608 | tf_op jit(solution)/shard_map/convert_element_type | solution.py:51
  (1 shorter events, 0.0 us)
Async XLA Ops:
  7.2 135.5 %reduce-scatter.2.cloned.1.call-start = ((), (), s32[]{:S(2)}) async-start(), calls=%async_computation.1 | async-start | bytes 8912896 | tf_op jit(solution)/shard_map/reduce_scatter | solution.py:31
  19.4 169.6 %copy-start = (f32[512,512]{1,0:T(8,128)S(1)}, f32[512,512]{1,0:T(8,128)}, u32[]{:S(2)}) copy-start(f32[512,512]{1,0:T(8,128)} %param.5) | copy-start | bytes 3145732
  19.4 169.6 %copy-start.1 = (f32[512,512]{1,0:T(8,128)S(1)}, f32[512,512]{1,0:T(8,128)}, u32[]{:S(2)}) copy-start(f32[512,512]{1,0:T(8,128)} %param.6) | copy-start | bytes 3145732
  19.4 172.6 %copy-start.2 = (s32[32,1]{0,1:T(1,128)S(1)}, s32[32,1]{0,1:T(1,128)}, u32[]{:S(2)}) copy-start(s32[32,1]{0,1:T(1,128)} %param.7) | copy-start | bytes 388
  19.4 221.7 %all-gather.2.cloned.1.call-start = ((), (), s32[]{:S(2)}) async-start(), calls=%async_computation.2 | async-start | bytes 8912896 | tf_op jit(solution)/shard_map/all_gather | solution.py:46
Sparse Core Ops, SparseCore 0:
  19.5 123.0 reduce-scatter.1
  192.1 48.9 all-gather.1
where the time goes:
time: 266 us
  waiting for transfers between devices  172 us (65%)
  blocking collectives  43.7 us (16%)
  other arithmetic  17.1 us (6%)
  between operations  14.8 us (6%)
  matrix products  13.4 us (5%)
  local copies, waits for them, and re-layouts  4.44 us (2%)
    reduce_scatter x1, waiting for transfers between devices, on_device(): lax.psum_scatter(local.astype(jnp.bfloat16), REPLICA, scatter_dimension=1...  123 us
    all_gather x1, waiting for transfers between devices, on_device(): piece = lax.all_gather(updated, SHARD, axis=0, tiled=True)  49 us
    psum x5, blocking collectives, over_axes(): return functools.reduce(lax.psum, axes, x)  43.7 us
    dot_general x1, matrix products, on_device(): jnp.einsum('bj,jrc->brc', picker, piece, preferred_element_type=jnp.float32)  13.4 us
    convert_element_type x1, other arithmetic, on_device(): local.astype(jnp.bfloat16)  10.1 us
  transfers between devices with their start and end apart: 2, of which 2 were waited for; matrix products, arithmetic and copies ran while one was open for 0% of the time, Pallas kernels for 0%

commit v1 on v0

v1 whole, which is shorter than its diff:
```python
import functools

import jax
import jax.numpy as jnp
from jax import lax
from jax.experimental import pallas as pl
from jax.experimental.pallas import tpu as pltpu
from jax.sharding import Mesh
from jax.sharding import PartitionSpec as P

BLOCK_ROWS = 128
SLOTS = 4
AXES = ("zh", "x", "y", "zl", "core")
MESH = pl.DeviceIdType.MESH
NC = 8
F32 = jnp.float32
BF16 = jnp.bfloat16


def comm_kernel(
    own, delta, master, momentum,
    ha, hb, mine, tot,
    d, xr, xd, xs, zr, zd, zs, ga, gb, b32, mst, mom, n1, n2,
    load_sem, mm_sem, out_sem,
    xrs, xrr, xds, xdr, xss, xsr,
    zrs, zrr, zds, zdr, zss, zsr,
    gs, gr, hs_sem, n1s, n1r, n2s, n2r,
):
    rows = d.shape[3]
    half = rows // 2
    cols = d.shape[4]
    zh, x, y = lax.axis_index("zh"), lax.axis_index("x"), lax.axis_index("y")
    zl, core = lax.axis_index("zl"), lax.axis_index("core")
    halves = (pl.ds(0, half), pl.ds(half, half))

    def ring(i):
        return lax.rem(i + 1, 4), lax.rem(i + 3, 4), lax.rem(i + 2, 4)

    xn, zn, yn = ring(x), ring(zh), ring(y)
    xp, xm, xo = xn
    zp, zm, zo = zn
    yp, ym, yo = yn
    zl2, core2 = 1 - zl, 1 - core

    barrier = pltpu.get_barrier_semaphore()
    for peer in (
        {"x": xp}, {"x": xm}, {"zh": zp}, {"zh": zm},
        {"y": yp}, {"y": ym}, {"zl": zl2}, {"core": core2},
    ):
        pl.semaphore_signal(barrier, inc=1, device_id=peer, device_id_type=MESH)

    def row_slice(c):
        return pl.ds(pl.multiple_of(c * rows, rows), rows)

    def load(c, carry):
        for i in range(4):
            for j in range(4):
                pltpu.make_async_copy(
                    delta.at[row_slice(c), pl.ds((i * 4 + j) * cols, cols)],
                    d.at[c, i, j],
                    load_sem.at[c],
                ).start()
        return carry

    def load_mm(c):
        return (
            pltpu.make_async_copy(master.at[row_slice(c)], mst.at[c], mm_sem.at[c, 0]),
            pltpu.make_async_copy(momentum.at[row_slice(c)], mom.at[c], mm_sem.at[c, 1]),
        )

    def start_mm(c, carry):
        for copy in load_mm(c):
            copy.start()
        return carry

    lax.fori_loop(0, 2, load, 0)
    lax.fori_loop(0, 2, start_mm, 0)
    lax.fori_loop(2, NC, load, 0)
    lax.fori_loop(2, NC, start_mm, 0)

    count = jnp.int32(0)
    shard = (y * 2 + zl) * 2 + core
    for b in range(own.shape[0]):
        count = count + (own[b] == shard).astype(jnp.int32)

    pl.semaphore_wait(barrier, 8)

    def send(src, dst, ss, rs, peer):
        return pltpu.make_async_remote_copy(
            src_ref=src, dst_ref=dst, send_sem=ss, recv_sem=rs, device_id=peer, device_id_type=MESH
        )

    class Phase:
        def __init__(self, axis, near, slab, recv, sems):
            self.axis, self.near, self.slab = axis, near, slab
            self.r, self.dd, self.s = recv
            self.rs, self.rr, self.ds, self.dr, self.ss, self.sr = sems

        def relay(self, c, h):
            return send(
                self.slab(c, self.near[2], h), self.r.at[c, h],
                self.rs.at[c, h], self.rr.at[c, h], {self.axis: self.near[h]},
            )

        def direct(self, c, h):
            return send(
                self.slab(c, self.near[h], 1 - h), self.dd.at[c, h],
                self.ds.at[c, h], self.dr.at[c, h], {self.axis: self.near[h]},
            )

        def summed(self, c, h):
            return send(
                self.slab(c, self.near[h], h), self.s.at[c, h],
                self.ss.at[c, h], self.sr.at[c, h], {self.axis: self.near[h]},
            )

        def all(self, c):
            return [f(c, h) for f in (self.relay, self.direct, self.summed) for h in range(2)]

    xph = Phase(
        "x", xn, lambda c, i, h: d.at[c, :, i, halves[h], :],
        (xr, xd, xs), (xrs, xrr, xds, xdr, xss, xsr),
    )
    zph = Phase(
        "zh", zn, lambda c, i, h: d.at[c, i, x, halves[h], :],
        (zr, zd, zs), (zrs, zrr, zds, zdr, zss, zsr),
    )

    def start_x(c):
        pltpu.make_async_copy(d.at[c], d.at[c], load_sem.at[c]).wait()
        for h in range(2):
            xph.relay(c, h).start()
        for h in range(2):
            xph.direct(c, h).start()

    def sum_x(c):
        for h in range(2):
            xph.relay(c, h).wait_recv()
            for k in range(4):
                to = xn[h]
                d[c, k, to, halves[h], :] = (
                    d[c, k, to, halves[h], :].astype(F32) + xr[c, h, k].astype(F32)
                ).astype(BF16)
            xph.summed(c, h).start()

    def end_x(c):
        for h in range(2):
            xph.direct(c, h).wait_recv()
        for h in range(2):
            xph.summed(c, h).wait_recv()
        for h in range(2):
            for k in range(4):
                d[c, k, x, halves[h], :] = (
                    d[c, k, x, halves[h], :].astype(F32)
                    + xs[c, h, k].astype(F32)
                    + xd[c, 1 - h, k].astype(F32)
                ).astype(BF16)
        for h in range(2):
            zph.relay(c, h).start()
        for h in range(2):
            zph.direct(c, h).start()

    def sum_z(c):
        for h in range(2):
            zph.relay(c, h).wait_recv()
            to = zn[h]
            d[c, to, x, halves[h], :] = (
                d[c, to, x, halves[h], :].astype(F32) + zr[c, h].astype(F32)
            ).astype(BF16)
            zph.summed(c, h).start()

    def g_copy(g, k, c, i):
        up, down = g.at[ym, :, c, halves[0], :], g.at[yp, :, c, halves[1], :]
        src = (
            g.at[y, zl, c], g.at[y, zl, c], g.at[y, zl, c],
            g.at[y, zl2, c], g.at[y, zl2, c], up, down, g.at[:, :, c],
        )[i]
        dst = (ha, hb)[k].at[:, :, core, row_slice(c), :] if i == 7 else src
        peer = (
            {"zl": zl2}, {"y": yp}, {"y": ym}, {"y": yp}, {"y": ym}, {"y": yp}, {"y": ym}, {"core": core2},
        )[i]
        return send(src, dst, gs.at[k, c, i], gr.at[k, c, i], peer)

    def g_local(g, k, c):
        return pltpu.make_async_copy(
            g.at[:, :, c], (ha, hb)[k].at[:, :, core, row_slice(c), :], hs_sem.at[k, c]
        )

    def g_start(g, k, c):
        for i in (0, 1, 2):
            g_copy(g, k, c, i).start()

    def g_second(g, k, c):
        g_copy(g, k, c, 0).wait_recv()
        for i in (3, 4):
            g_copy(g, k, c, i).start()

    def g_third(g, k, c):
        for i in (1, 2, 3, 4):
            g_copy(g, k, c, i).wait_recv()
        for i in (5, 6):
            g_copy(g, k, c, i).start()

    def g_last(g, k, c):
        for i in (5, 6):
            g_copy(g, k, c, i).wait_recv()
        g_copy(g, k, c, 7).start()
        g_local(g, k, c).start()

    def mine_out(c):
        return pltpu.make_async_copy(b32.at[c], mine.at[row_slice(c)], out_sem.at[c])

    n1[zh * 4 + x] = jnp.zeros((8, 128), F32)

    def end_z(c):
        for h in range(2):
            zph.direct(c, h).wait_recv()
        for h in range(2):
            zph.summed(c, h).wait_recv()
        slot = (c * rows) // BLOCK_ROWS
        for h in range(2):
            value = (
                d[c, zh, x, halves[h], :].astype(F32)
                + zs[c, h].astype(F32)
                + zd[c, 1 - h].astype(F32)
            ) * F32(0.0625)
            value = jnp.where(slot < count, value, F32(0.0))
            b32[c, halves[h], :] = value
            gb[y, zl, c, halves[h], :] = value.astype(BF16)
            square = jnp.sum((value * value).reshape(half // 8, 8, cols), axis=0)
            part = square[:, :128]
            for k in range(1, cols // 128):
                part = part + square[:, k * 128:(k + 1) * 128]
            n1[zh * 4 + x] = n1[zh * 4 + x] + part
        g_start(gb, 1, c)
        mine_out(c).start()

    def start_a(c):
        for copy in load_mm(c):
            copy.wait()
        for h in range(2):
            ga[y, zl, c, halves[h], :] = (
                mst[c, halves[h], :] - F32(0.567) * mom[c, halves[h], :]
            ).astype(BF16)
        g_start(ga, 0, c)

    def at(t, lag, f):
        @pl.when((t >= lag) & (t < NC + lag))
        def _():
            f(t - lag)

    def loop_body(t, carry):
        at(t, 0, start_x)
        at(t, 1, sum_x)
        at(t, 2, end_x)
        at(t, 3, sum_z)
        at(t, 4, end_z)
        at(t, 0, start_a)
        at(t, 1, functools.partial(g_second, ga, 0))
        at(t, 2, functools.partial(g_third, ga, 0))
        at(t, 3, functools.partial(g_last, ga, 0))
        at(t, 5, functools.partial(g_second, gb, 1))
        at(t, 6, functools.partial(g_third, gb, 1))
        at(t, 7, functools.partial(g_last, gb, 1))
        return carry

    def norm1(i):
        r = zh * 4 + x
        q = lax.rem(r + i, 16)
        return send(n1.at[r], n1.at[r], n1s.at[i], n1r.at[i], {"zh": q // 4, "x": lax.rem(q, 4)})

    def norm2(i):
        q = lax.rem(shard + i, 16)
        return send(
            n2.at[shard], n2.at[shard], n2s.at[i], n2r.at[i],
            {"y": q // 4, "zl": lax.rem(q // 2, 2), "core": lax.rem(q, 2)},
        )

    lax.fori_loop(0, NC + 4, loop_body, 0)
    for i in range(1, 16):
        norm1(i).start()
    g_second(gb, 1, NC - 1)
    g_third(gb, 1, NC - 2)
    g_last(gb, 1, NC - 3)
    g_third(gb, 1, NC - 1)
    g_last(gb, 1, NC - 2)
    for i in range(1, 16):
        norm1(i).wait_recv()
    n2[shard] = jnp.sum(n1[...], axis=0)
    for i in range(1, 16):
        norm2(i).start()
    g_last(gb, 1, NC - 1)
    for i in range(1, 16):
        norm2(i).wait_recv()
    tot[...] = jnp.sum(n2[...], axis=0)

    for i in range(1, 16):
        norm1(i).wait_send()
        norm2(i).wait_send()

    def drain(c, carry):
        for copy in xph.all(c) + zph.all(c):
            copy.wait_send()
        for k, g in ((0, ga), (1, gb)):
            for i in range(8):
                g_copy(g, k, c, i).wait_send()
            g_copy(g, k, c, 7).wait_recv()
            g_local(g, k, c).wait()
        mine_out(c).wait()
        return carry

    lax.fori_loop(0, NC, drain, 0)


def finish_kernel(
    own, tot, ha, hb, mine, master, momentum,
    master_out, momentum_out, params,
    a, b, p, g, m, v, mo, vo, counts, sem, gsem, psem, osem,
):
    blocks = own.shape[0]
    shard = (lax.axis_index("y") * 2 + lax.axis_index("zl")) * 2 + lax.axis_index("core")
    for k in range(16):
        counts[k] = 0
    for src, dst, s in ((mine, g, 0), (master, m, 1), (momentum, v, 2)):
        pltpu.make_async_copy(src, dst, gsem.at[s]).start()

    def begin(i, carry):
        k = own[i]
        j = counts[k]
        counts[k] = j + 1
        flat = k * SLOTS + j
        pltpu.make_async_copy(ha.at[flat], a.at[i], sem.at[0, i]).start()
        pltpu.make_async_copy(hb.at[flat], b.at[i], sem.at[1, i]).start()
        return carry

    lax.fori_loop(0, blocks, begin, 0)
    limit = 0.5 * jnp.sqrt(jnp.full((1, 1), blocks * BLOCK_ROWS * params.shape[1] * 16, F32))
    total = jnp.sum(jnp.sum(tot[...], axis=0, keepdims=True), axis=1, keepdims=True)
    factor = jnp.minimum(F32(1.0), limit / (jnp.sqrt(total) + F32(1e-06)))
    scale = F32(1.33) * factor

    for src, dst, s in ((mine, g, 0), (master, m, 1), (momentum, v, 2)):
        pltpu.make_async_copy(src, dst, gsem.at[s]).wait()
    count = counts[shard]

    def update(j, carry):
        r = pl.ds(pl.multiple_of(j * 32, 32), 32)
        live = j // 4 < count
        grad = factor * g[r, :]
        old = v[r, :]
        new = jnp.where(live, F32(0.9) * old + grad, old)
        w = m[r, :]
        vo[r, :] = new
        mo[r, :] = jnp.where(live, w - F32(0.7) * (grad + F32(0.9) * new), w)
        return carry

    lax.fori_loop(0, g.shape[0] // 32, update, 0)
    pltpu.make_async_copy(mo, master_out, osem.at[0]).start()
    pltpu.make_async_copy(vo, momentum_out, osem.at[1]).start()

    def out(i):
        r = pl.ds(pl.multiple_of(i * BLOCK_ROWS, BLOCK_ROWS), BLOCK_ROWS)
        return pltpu.make_async_copy(p.at[i], params.at[r], psem.at[i])

    def block(i, carry):
        pltpu.make_async_copy(ha.at[0], a.at[i], sem.at[0, i]).wait()
        pltpu.make_async_copy(hb.at[0], b.at[i], sem.at[1, i]).wait()
        for k in range(4):
            r = pl.ds(k * 32, 32)
            p[i, r, :] = (a[i, r, :].astype(F32) - scale * b[i, r, :].astype(F32)).astype(BF16)
        out(i).start()
        return carry

    lax.fori_loop(0, blocks, block, 0)
    pltpu.make_async_copy(mo, master_out, osem.at[0]).wait()
    pltpu.make_async_copy(vo, momentum_out, osem.at[1]).wait()

    def end(i, carry):
        out(i).wait()
        return carry

    lax.fori_loop(0, blocks, end, 0)


def on_device(deltas, master, momentum, block_owner):
    rows, cols = master.shape
    part = rows // NC
    half = part // 2
    own = block_owner.reshape(-1)
    blocks = own.shape[0]
    any_spec = pl.BlockSpec(memory_space=pl.ANY)
    vmem = pl.BlockSpec(memory_space=pltpu.VMEM)
    smem = pl.BlockSpec(memory_space=pltpu.SMEM)
    sem = pltpu.SemaphoreType.DMA
    gathered = jax.ShapeDtypeStruct((4, 2, 2, rows, cols), BF16)
    ha, hb, mine, tot = pl.pallas_call(
        comm_kernel,
        name="reduce_gather",
        out_shape=(
            gathered, gathered,
            jax.ShapeDtypeStruct((rows, cols), F32),
            jax.ShapeDtypeStruct((8, 128), F32),
        ),
        in_specs=[smem, any_spec, any_spec, any_spec],
        out_specs=(any_spec, any_spec, any_spec, vmem),
        scratch_shapes=(
            [pltpu.VMEM((NC, 4, 4, part, cols), BF16)]
            + [pltpu.VMEM((NC, 2, 4, half, cols), BF16)] * 3
            + [pltpu.VMEM((NC, 2, half, cols), BF16)] * 3
            + [pltpu.VMEM((4, 2, NC, part, cols), BF16)] * 2
            + [pltpu.VMEM((NC, part, cols), F32)] * 3
            + [pltpu.VMEM((16, 8, 128), F32)] * 2
            + [sem((NC,)), sem((NC, 2)), sem((NC,))]
            + [sem((NC, 2))] * 12
            + [sem((2, NC, 8))] * 2
            + [sem((2, NC))]
            + [sem((16,))] * 4
        ),
        compiler_params=pltpu.CompilerParams(
            collective_id=0, has_side_effects=True, vmem_limit_bytes=60 * 1024 * 1024
        ),
    )(own, deltas.reshape(rows, -1), master, momentum)
    slots = 16 * SLOTS
    ha = ha.reshape(slots, BLOCK_ROWS, cols)
    hb = hb.reshape(slots, BLOCK_ROWS, cols)
    return pl.pallas_call(
        finish_kernel,
        name="finish",
        out_shape=(
            jax.ShapeDtypeStruct((rows, cols), F32),
            jax.ShapeDtypeStruct((rows, cols), F32),
            jax.ShapeDtypeStruct((blocks * BLOCK_ROWS, cols), BF16),
        ),
        in_specs=[smem, vmem] + [any_spec] * 5,
        out_specs=(any_spec, any_spec, any_spec),
        scratch_shapes=(
            [pltpu.VMEM((blocks, BLOCK_ROWS, cols), BF16)] * 3
            + [pltpu.VMEM((rows, cols), F32)] * 5
            + [pltpu.SMEM((16,), jnp.int32)]
            + [sem((2, blocks)), sem((3,)), sem((blocks,)), sem((2,))]
        ),
        compiler_params=pltpu.CompilerParams(vmem_limit_bytes=60 * 1024 * 1024),
    )(own, tot, ha, hb, mine, master, momentum)


def solution(mesh):
    finer = Mesh(mesh.devices.reshape(4, 4, 4, 2, 2), AXES)
    replica, shard = AXES[:2], AXES[2:]
    in_specs = (P(replica, shard, None), P(shard, replica), P(shard, replica), P())
    out_specs = (P(shard, replica), P(shard, replica), P(None, replica))
    return jax.shard_map(
        on_device, mesh=finer, in_specs=in_specs, out_specs=out_specs, check_vma=False
    )
```

time: 266 us -> 124 us (0.47)
  waiting for transfers between devices: 172 us -> 0 us
  Pallas kernels: 0 us -> 123 us
  blocking collectives: 43.7 us -> 0 us
  other arithmetic: 17.1 us -> 0 us
  between operations: 14.8 us -> 0.64 us
  matrix products: 13.4 us -> 0 us
  local copies, waits for them, and re-layouts: 4.44 us -> 0 us
    reduce_scatter x1 -> x0, waiting for transfers between devices: 123 us -> none  [on_device(): lax.psum_scatter(local.astype(jnp.bfloat16), REPLICA, scatter_dimension=1...]
    pallas_call x0 -> x2, Pallas kernels: none -> 123 us  [the longest x1 115 us: on_device(): pl.pallas_call(comm_kernel, name='reduce_gather', out_shape=(gathered, ga...]
    all_gather x1 -> x0, waiting for transfers between devices: 49 us -> none  [on_device(): piece = lax.all_gather(updated, SHARD, axis=0, tiled=True)]
    psum x5 -> x0, blocking collectives: 43.7 us -> none  [over_axes(): return functools.reduce(lax.psum, axes, x)]
    dot_general x1 -> x0, matrix products: 13.4 us -> none  [on_device(): jnp.einsum('bj,jrc->brc', picker, piece, preferred_element_type=jnp.float32)]
    convert_element_type x2 -> x0, other arithmetic: 13.1 us -> none  [the longest x1 10.1 us: on_device(): local.astype(jnp.bfloat16)]
    convert_element_type x1 -> x0, local copies, waits for them, and re-layouts: 4.36 us -> none  [on_device(): params = placed.astype(jnp.bfloat16).reshape(blocks * BLOCK_ROWS, cols)]
    reduce_sum x3 -> x0, other arithmetic: 3.39 us -> none  [the longest x1 1.92 us: on_device(): total = over_axes(jnp.sum(avg * avg), REPLICA_SHARD)]
  transfers between devices with their start and end apart: 2 -> 0, of which waited for: 2 -> 0; matrix products, arithmetic and copies ran while one was open for 0% -> 0% of each run, Pallas kernels for 0% -> 0%
where the time goes in v1:
time: 124 us
  Pallas kernels  123 us (99%)
    pallas_call x1, Pallas kernels, on_device(): pl.pallas_call(comm_kernel, name='reduce_gather', out_shape=(gathered, ga...  115 us
    pallas_call x1, Pallas kernels, on_device(): pl.pallas_call(finish_kernel, name='finish', out_shape=(jax.ShapeDtypeStr...  8.47 us

profile of v1, /device:TPU:1, one launch (start us, length us, event | category | flops | bytes accessed | tf_op | source)
XLA Modules:
  0.0 123.8 jit_solution(14870239439032267869)
XLA Ops:
  0.6 114.7 %reduce_gather.1 = (bf16[4,2,2,512,512]{4,3,2,1,0:T(8,128)(2,1)}, bf16[4,2,2,512,512]{4,3,2,1,0:T(8,128)(2,1)}, f32[512,512]{1,0:T(8,128)}, f32[8,128]{1,0:T(8,128)}) custom-call(s32[32]{0:T(128)} %bitcast.7, bf16[512,8192]{1,0:T(8,128)(2,1)} %bitcast.6, f32[512,512]{1,0:T(8,128)} %master.3, f32[512,512]{1,0:T(8,128)} %momentum.3), custom_call_target="tpu_custom_call" | custom-call | tf_op jit(solution)/shard_map/reduce_gather/pallas_call | solution.py:396
  115.3 8.5 %finish.1 = (f32[512,512]{1,0:T(8,128)}, f32[512,512]{1,0:T(8,128)}, bf16[4096,512]{1,0:T(8,128)(2,1)}) custom-call(s32[32]{0:T(128)} %bitcast.8, f32[8,128]{1,0:T(8,128)} %get-tuple-element.7.tot, bf16[64,128,512]{2,1,0:T(8,128)(2,1)} %bitcast.4, bf16[64,128,512]{2,1,0:T(8,128)(2,1)} %bitcast.5, f32[512,512]{1,0:T(8,128)} %get-tuple-element.10.mine, ...), custom_call_target="tpu_custom_call" | custom-call | tf_op jit(solution)/shard_map/finish/pallas_call | solution.py:426

commit v2 on v1

v2 whole, which is shorter than its diff:
```python
import functools

import jax
import jax.numpy as jnp
from jax import lax
from jax.experimental import pallas as pl
from jax.experimental.pallas import tpu as pltpu
from jax.sharding import Mesh
from jax.sharding import PartitionSpec as P

BLOCK_ROWS = 128
SLOTS = 4
HALF_BLOCK = 64
AXES = ("zh", "x", "y", "zl", "core")
MESH = pl.DeviceIdType.MESH
R = 32
LA = 1
F32 = jnp.float32
BF16 = jnp.bfloat16


def comm_kernel(
    nc,
    own, delta, master, momentum,
    ha, hb, tot,
    d, xt, xr, xd, xs, zr, zd, zs, ga, gb, mst, mom, axs, axr, acc, n1, n2,
    load_sem, ex_sem, mm_sem, xt_sem, ax_sem,
    xrs, xrr, xds, xdr, xss, xsr,
    zrs, zrr, zds, zdr, zss, zsr,
    gs, gr, hs_sem, n1s, n1r, n2s, n2r,
):
    chunks = d.shape[0]
    extra = chunks - nc
    per_block = BLOCK_ROWS // R
    half = R // 2
    cols = master.shape[2]
    zh, x, y = lax.axis_index("zh"), lax.axis_index("x"), lax.axis_index("y")
    zl, core = lax.axis_index("zl"), lax.axis_index("core")
    halves = (pl.ds(0, half), pl.ds(half, half))
    replica = zh * 4 + x
    shard = (y * 2 + zl) * 2 + core
    twin = (y * 2 + zl) * 2 + 1 - core

    def ring(i):
        return lax.rem(i + 1, 4), lax.rem(i + 3, 4), lax.rem(i + 2, 4)

    def lanes(i):
        return pl.ds(pl.multiple_of(i * cols, cols), cols)

    xn, zn, yn = ring(x), ring(zh), ring(y)
    yp, ym, yo = yn
    zl2, core2 = 1 - zl, 1 - core

    barrier = pltpu.get_barrier_semaphore()
    for peer in (
        {"x": xn[0]}, {"x": xn[1]}, {"zh": zn[0]}, {"zh": zn[1]},
        {"y": yp}, {"y": ym}, {"zl": zl2}, {"core": core2},
    ):
        pl.semaphore_signal(barrier, inc=1, device_id=peer, device_id_type=MESH)

    def load(c):
        for k in range(4):
            pltpu.make_async_copy(
                delta.at[c, :, pl.ds(k * 4 * cols, 4 * cols)], d.at[c, k], load_sem.at[c]
            ).start()

    for c in range(LA):
        load(c)
    if extra:
        for k in range(4):
            pltpu.make_async_copy(
                delta.at[pl.ds(nc, extra), :, pl.ds(k * 4 * cols, 4 * cols)],
                d.at[pl.ds(nc, extra), k], ex_sem,
            ).start()
    get_m = pltpu.make_async_copy(master, mst, mm_sem.at[0])
    get_v = pltpu.make_async_copy(momentum, mom, mm_sem.at[1])
    get_m.start()
    get_v.start()

    def load_next(c, carry):
        load(c)
        return carry

    lax.fori_loop(LA, nc, load_next, 0)

    count, twin_count = jnp.int32(0), jnp.int32(0)
    for b in range(own.shape[0]):
        count = count + (own[b] == shard).astype(jnp.int32)
        twin_count = twin_count + (own[b] == twin).astype(jnp.int32)

    def spare(c):
        i = c - per_block * count
        return i, (i >= 0) & (i < extra), jnp.clip(i, 0, max(extra - 1, 0))

    def is_live(c):
        i, inside, _ = spare(c)
        live = c < per_block * count
        if extra:
            live = live | (inside & (i + nc < per_block * twin_count))
        return live

    acc[...] = jnp.zeros_like(acc)
    pl.semaphore_wait(barrier, 8)

    def send(src, dst, ss, rs, peer):
        return pltpu.make_async_remote_copy(
            src_ref=src, dst_ref=dst, send_sem=ss, recv_sem=rs, device_id=peer, device_id_type=MESH
        )

    def xt_copy():
        return send(d.at[pl.ds(nc, extra)], xt, xt_sem.at[0], xt_sem.at[1], {"core": core2})

    def ax_copy():
        return send(axs, axr, ax_sem.at[0], ax_sem.at[1], {"core": core2})

    class Phase:
        def __init__(self, axis, near, slab, recv, sems):
            self.axis, self.near, self.slab = axis, near, slab
            self.r, self.dd, self.s = recv
            self.rs, self.rr, self.ds, self.dr, self.ss, self.sr = sems

        def relay(self, c, h):
            return send(
                self.slab(c, self.near[2], h), self.r.at[c, h],
                self.rs.at[c, h], self.rr.at[c, h], {self.axis: self.near[h]},
            )

        def direct(self, c, h):
            return send(
                self.slab(c, self.near[h], 1 - h), self.dd.at[c, h],
                self.ds.at[c, h], self.dr.at[c, h], {self.axis: self.near[h]},
            )

        def summed(self, c, h):
            return send(
                self.slab(c, self.near[h], h), self.s.at[c, h],
                self.ss.at[c, h], self.sr.at[c, h], {self.axis: self.near[h]},
            )

        def wait_sends(self, c):
            for f in (self.relay, self.direct, self.summed):
                for h in range(2):
                    f(c, h).wait_send()

    xph = Phase(
        "x", xn, lambda c, i, h: d.at[c, :, halves[h], lanes(i)],
        (xr, xd, xs), (xrs, xrr, xds, xdr, xss, xsr),
    )
    zph = Phase(
        "zh", zn, lambda c, i, h: d.at[c, i, halves[h], lanes(x)],
        (zr, zd, zs), (zrs, zrr, zds, zdr, zss, zsr),
    )

    def start_x(c, fixed=False):
        pltpu.make_async_copy(d.at[c], d.at[c], load_sem.at[c]).wait()
        if extra and not fixed:
            _, use, at = spare(c)

            @pl.when(c == per_block)
            def _():
                xt_copy().wait_recv()

            @pl.when(c >= per_block)
            def _():
                for k in range(4):
                    d[c, k] = jnp.where(use, xt[at, k], d[c, k])
        for h in range(2):
            xph.relay(c, h).start()
        for h in range(2):
            xph.direct(c, h).start()

    def sum_x(c):
        for h in range(2):
            xph.relay(c, h).wait_recv()
            for k in range(4):
                to = lanes(xn[h])
                d[c, k, halves[h], to] = (
                    d[c, k, halves[h], to].astype(F32) + xr[c, h, k].astype(F32)
                ).astype(BF16)
            xph.summed(c, h).start()

    def end_x(c):
        for h in range(2):
            xph.direct(c, h).wait_recv()
        for h in range(2):
            xph.summed(c, h).wait_recv()
        for h in range(2):
            for k in range(4):
                d[c, k, halves[h], lanes(x)] = (
                    d[c, k, halves[h], lanes(x)].astype(F32)
                    + xs[c, h, k].astype(F32)
                    + xd[c, 1 - h, k].astype(F32)
                ).astype(BF16)
        for h in range(2):
            zph.relay(c, h).start()
        for h in range(2):
            zph.direct(c, h).start()

    def sum_z(c):
        for h in range(2):
            zph.relay(c, h).wait_recv()
            to = zn[h]
            d[c, to, halves[h], lanes(x)] = (
                d[c, to, halves[h], lanes(x)].astype(F32) + zr[c, h].astype(F32)
            ).astype(BF16)
            zph.summed(c, h).start()

    def place(h, c):
        return h.at[:, :, core, pl.ds(pl.multiple_of(c * R, R), R), :]

    def g_copy(k, c, i):
        g = (ga, gb)[k]
        up, down = g.at[ym, :, c, halves[0], :], g.at[yp, :, c, halves[1], :]
        src = (
            g.at[y, zl, c], g.at[y, zl, c], g.at[y, zl, c],
            g.at[y, zl2, c], g.at[y, zl2, c], up, down, g.at[:, :, c],
        )[i]
        dst = place((ha, hb)[k], c) if i == 7 else src
        peer = (
            {"zl": zl2}, {"y": yp}, {"y": ym}, {"y": yp}, {"y": ym}, {"y": yp}, {"y": ym}, {"core": core2},
        )[i]
        return send(src, dst, gs.at[k, c, i], gr.at[k, c, i], peer)

    def g_local(k, c):
        return pltpu.make_async_copy((ga, gb)[k].at[:, :, c], place((ha, hb)[k], c), hs_sem.at[k, c])

    def g_start(k, c):
        for i in (0, 1, 2):
            g_copy(k, c, i).start()

    def g_second(k, c):
        g_copy(k, c, 0).wait_recv()
        for i in (3, 4):
            g_copy(k, c, i).start()

    def g_third(k, c):
        for i in (1, 2, 3, 4):
            g_copy(k, c, i).wait_recv()
        for i in (5, 6):
            g_copy(k, c, i).start()

    def g_last(k, c):
        for i in (5, 6):
            g_copy(k, c, i).wait_recv()
        g_copy(k, c, 7).start()
        g_local(k, c).start()

    def g_drain(k, c):
        for i in range(8):
            g_copy(k, c, i).wait_send()
        g_copy(k, c, 7).wait_recv()
        g_local(k, c).wait()

    def end_z(c):
        for h in range(2):
            zph.direct(c, h).wait_recv()
        for h in range(2):
            zph.summed(c, h).wait_recv()
        live = is_live(c)
        for h in range(2):
            value = (
                d[c, zh, halves[h], lanes(x)].astype(F32)
                + zs[c, h].astype(F32)
                + zd[c, 1 - h].astype(F32)
            ) * F32(0.0625)
            value = jnp.where(live, value, F32(0.0))
            gb[y, zl, c, halves[h], :] = value.astype(BF16)
            square = jnp.sum((value * value).reshape(half // 8, 8, cols), axis=0)
            part = square[:, :128]
            for k in range(1, cols // 128):
                part = part + square[:, k * 128:(k + 1) * 128]
            acc[...] += part
        g_start(1, c)

    def a_of(c, r):
        return (mst[c, r, :] - F32(0.567) * mom[c, r, :]).astype(BF16)

    def start_a(c, fixed=False):
        for r in halves:
            value = a_of(c, r)
            if extra and not fixed:
                _, use, at = spare(c)
                value = jnp.where(use, axr[at, r, :], value)
            ga[y, zl, c, r, :] = value
        g_start(0, c)

    def at(t, lag, f):
        @pl.when((t >= lag) & (t < nc + lag))
        def _():
            f(t - lag)

    def loop_body(t, carry):
        at(t, -LA, start_x)
        at(t, -LA, start_a)
        at(t, 0, sum_x)
        at(t, 1 - LA, functools.partial(g_second, 0))
        at(t, 1, end_x)
        at(t, 2 - LA, functools.partial(g_third, 0))
        at(t, 2, sum_z)
        at(t, 3, end_z)
        at(t, 3 - LA, functools.partial(g_last, 0))
        at(t, 4, functools.partial(g_second, 1))
        at(t, 5, functools.partial(g_third, 1))
        at(t, 6, functools.partial(g_last, 1))
        return carry

    def norm1(i):
        q = lax.rem(replica + i, 16)
        return send(
            n1.at[replica], n1.at[replica], n1s.at[i], n1r.at[i],
            {"zh": q // 4, "x": lax.rem(q, 4)},
        )

    def norm2(i):
        q = lax.rem(shard + i, 16)
        return send(
            n2.at[shard], n2.at[shard], n2s.at[i], n2r.at[i],
            {"y": q // 4, "zl": lax.rem(q // 2, 2), "core": lax.rem(q, 2)},
        )

    for c in range(LA):
        start_x(c, fixed=True)
    get_m.wait()
    get_v.wait()
    if extra:
        pltpu.make_async_copy(
            d.at[pl.ds(nc, extra)], d.at[pl.ds(nc, extra)], ex_sem
        ).wait()
        xt_copy().start()
        for e in range(extra):
            axs[e] = a_of(nc + e, slice(None))
        ax_copy().start()
    for c in range(LA):
        start_a(c, fixed=True)
    if extra:
        ax_copy().wait_recv()
    for t in range(1 - LA, 0):
        for lag, f in ((1, g_second), (2, g_third), (3, g_last)):
            if t - (lag - LA) >= 0:
                f(0, t - (lag - LA))
    lax.fori_loop(0, nc + 3, loop_body, 0)

    n1[replica] = jnp.sum(acc[...], axis=0, keepdims=True)
    for i in range(1, 16):
        norm1(i).start()
    g_second(1, nc - 1)
    g_third(1, nc - 2)
    g_last(1, nc - 3)

    def drain1(c, carry):
        xph.wait_sends(c)
        zph.wait_sends(c)
        return carry

    lax.fori_loop(0, nc, drain1, 0)
    if extra:
        xt_copy().wait_send()
        ax_copy().wait_send()
    g_third(1, nc - 1)
    g_last(1, nc - 2)
    for i in range(1, 16):
        norm1(i).wait_recv()
    n2[shard] = jnp.sum(n1[...], axis=0)
    for i in range(1, 16):
        norm2(i).start()

    def drain2(c, carry):
        g_drain(0, c)
        return carry

    def drain3(c, carry):
        g_drain(1, c)
        return carry

    g_last(1, nc - 1)
    lax.fori_loop(0, nc, drain2, 0)
    lax.fori_loop(0, nc - 2, drain3, 0)
    for i in range(1, 16):
        norm1(i).wait_send()
    for i in range(1, 16):
        norm2(i).wait_recv()
    tot[...] = jnp.sum(n2[...], axis=0)
    for i in range(1, 16):
        norm2(i).wait_send()
    lax.fori_loop(nc - 2, nc, drain3, 0)


def finish_kernel(
    own, size, tot, ha, hb, master, momentum,
    master_out, momentum_out, params,
    a, b, p, g, m, v, mo, vo, counts, slots, sem, gsem, msem, psem, osem,
):
    blocks = own.shape[0]
    per = params.shape[0] // blocks // HALF_BLOCK
    shard = (lax.axis_index("y") * 2 + lax.axis_index("zl")) * 2 + lax.axis_index("core")
    limit_of = SLOTS * per
    n = size[0]
    pltpu.make_async_copy(master, m, msem.at[0]).start()
    pltpu.make_async_copy(momentum, v, msem.at[1]).start()
    for k in range(16):
        counts[k] = 0
        slots[k] = 0
    for i in range(blocks):
        counts[own[i]] = counts[own[i]] + 1

    def flat(k, q):
        other = k + 1 - 2 * lax.rem(k, 2)
        return jnp.where(q < n, k * limit_of + q, other * limit_of + q - n + per * counts[other])

    def begin(i, carry):
        k = own[i]
        j = slots[k]
        slots[k] = j + 1
        for r in range(per):
            f = flat(k, j * per + r)
            pltpu.make_async_copy(ha.at[f], a.at[i, r], sem.at[0, i, r]).start()
            pltpu.make_async_copy(hb.at[f], b.at[i, r], sem.at[1, i, r]).start()
        return carry

    lax.fori_loop(0, blocks, begin, 0)
    count = counts[shard]
    for q in range(limit_of):
        f = jnp.where(q < per * count, flat(shard, q), 0)
        pltpu.make_async_copy(hb.at[f], g.at[q], gsem.at[q]).start()
    limit = 0.5 * jnp.sqrt(jnp.full((1, 1), params.shape[0] * params.shape[1] * 16, F32))
    total = jnp.sum(tot[...], axis=1, keepdims=True)
    factor = jnp.minimum(F32(1.0), limit / (jnp.sqrt(total) + F32(1e-06)))
    scale = F32(1.33) * factor

    def out(i):
        r = pl.ds(pl.multiple_of(i * BLOCK_ROWS, BLOCK_ROWS), BLOCK_ROWS)
        return pltpu.make_async_copy(p.at[i], params.at[r], psem.at[i])

    def block(i, carry):
        for r in range(per):
            pltpu.make_async_copy(ha.at[0], a.at[i, r], sem.at[0, i, r]).wait()
            pltpu.make_async_copy(hb.at[0], b.at[i, r], sem.at[1, i, r]).wait()
            for k in range(2):
                w = pl.ds(k * 32, 32)
                p[i, pl.ds(r * HALF_BLOCK + k * 32, 32), :] = (
                    a[i, r, w, :].astype(F32) - scale * b[i, r, w, :].astype(F32)
                ).astype(BF16)
        out(i).start()
        return carry

    lax.fori_loop(0, blocks, block, 0)
    pltpu.make_async_copy(master, m, msem.at[0]).wait()
    pltpu.make_async_copy(momentum, v, msem.at[1]).wait()

    def update(q, carry):
        pltpu.make_async_copy(hb.at[0], g.at[q], gsem.at[q]).wait()
        live = q < per * count
        for k in range(2):
            w = pl.ds(k * 32, 32)
            r = pl.ds(pl.multiple_of(q * HALF_BLOCK + k * 32, 32), 32)
            grad = factor * g[q, w, :].astype(F32)
            old = v[r, :]
            new = jnp.where(live, F32(0.9) * old + grad, old)
            z = m[r, :]
            vo[r, :] = new
            mo[r, :] = jnp.where(live, z - F32(0.7) * (grad + F32(0.9) * new), z)
        return carry

    lax.fori_loop(0, limit_of, update, 0)
    put_m = pltpu.make_async_copy(mo, master_out, osem.at[0])
    put_v = pltpu.make_async_copy(vo, momentum_out, osem.at[1])
    put_m.start()
    put_v.start()

    def end(i, carry):
        out(i).wait()
        return carry

    lax.fori_loop(0, blocks, end, 0)
    put_m.wait()
    put_v.wait()


def size_kernel(own, size):
    chips = [jnp.int32(0)] * 8
    for i in range(own.shape[0]):
        chip = own[i] // 2
        chips = [n + (chip == k).astype(jnp.int32) for k, n in enumerate(chips)]
    most = functools.reduce(jnp.maximum, chips)
    size[0] = jnp.maximum(most, SIZES[0])


SIZES = (5, 6, 7, 8)


def on_device(deltas, master, momentum, block_owner):
    rows, cols = master.shape
    width = deltas.shape[2]
    chunks = rows // R
    half = R // 2
    own = block_owner.reshape(-1)
    blocks = own.shape[0]
    any_spec = pl.BlockSpec(memory_space=pl.ANY)
    vmem = pl.BlockSpec(memory_space=pltpu.VMEM)
    smem = pl.BlockSpec(memory_space=pltpu.SMEM)
    sem = pltpu.SemaphoreType.DMA
    gathered = jax.ShapeDtypeStruct((4, 2, 2, rows, cols), BF16)

    def comm(size, ident):
        nc = size * HALF_BLOCK // R
        extra = max(chunks - nc, 1)
        call = pl.pallas_call(
            functools.partial(comm_kernel, nc),
            name=f"reduce_gather_{size}",
            out_shape=(gathered, gathered, jax.ShapeDtypeStruct((1, 128), F32)),
            in_specs=[smem, any_spec, any_spec, any_spec],
            out_specs=(any_spec, any_spec, vmem),
            scratch_shapes=(
                [pltpu.VMEM((chunks, 4, R, 4 * cols), BF16)]
                + [pltpu.VMEM((extra, 4, R, 4 * cols), BF16)]
                + [pltpu.VMEM((nc, 2, 4, half, cols), BF16)] * 3
                + [pltpu.VMEM((nc, 2, half, cols), BF16)] * 3
                + [pltpu.VMEM((4, 2, nc, R, cols), BF16)] * 2
                + [pltpu.VMEM((chunks, R, cols), F32)] * 2
                + [pltpu.VMEM((extra, R, cols), BF16)] * 2
                + [pltpu.VMEM((8, 128), F32)]
                + [pltpu.VMEM((16, 1, 128), F32)] * 2
                + [sem((nc,)), sem, sem((2,)), sem((2,)), sem((2,))]
                + [sem((nc, 2))] * 12
                + [sem((2, nc, 8))] * 2
                + [sem((2, nc))]
                + [sem((16,))] * 4
            ),
            compiler_params=pltpu.CompilerParams(
                collective_id=ident, has_side_effects=True, vmem_limit_bytes=60 * 1024 * 1024
            ),
        )
        return lambda o, d, m, v: call(o, d, m, v)

    size = pl.pallas_call(
        size_kernel,
        name="size",
        out_shape=jax.ShapeDtypeStruct((1,), jnp.int32),
        in_specs=[smem],
        out_specs=smem,
    )(own)
    operands = (
        own,
        deltas.reshape(chunks, R, width),
        master.reshape(chunks, R, cols),
        momentum.reshape(chunks, R, cols),
    )
    branches = [comm(s, i) for i, s in enumerate(SIZES)]
    if len(branches) == 1:
        ha, hb, tot = branches[0](*operands)
    else:
        ha, hb, tot = lax.switch(size[0] - SIZES[0], branches, *operands)
    parts = 16 * rows // HALF_BLOCK
    ha = ha.reshape(parts, HALF_BLOCK, cols)
    hb = hb.reshape(parts, HALF_BLOCK, cols)
    per = BLOCK_ROWS // HALF_BLOCK
    return pl.pallas_call(
        finish_kernel,
        name="finish",
        out_shape=(
            jax.ShapeDtypeStruct((rows, cols), F32),
            jax.ShapeDtypeStruct((rows, cols), F32),
            jax.ShapeDtypeStruct((blocks * BLOCK_ROWS, cols), BF16),
        ),
        in_specs=[smem, smem, vmem] + [any_spec] * 4,
        out_specs=(any_spec, any_spec, any_spec),
        scratch_shapes=(
            [pltpu.VMEM((blocks, per, HALF_BLOCK, cols), BF16)] * 2
            + [pltpu.VMEM((blocks, BLOCK_ROWS, cols), BF16)]
            + [pltpu.VMEM((SLOTS * per, HALF_BLOCK, cols), BF16)]
            + [pltpu.VMEM((rows, cols), F32)] * 4
            + [pltpu.SMEM((16,), jnp.int32)] * 2
            + [sem((2, blocks, per)), sem((SLOTS * per,)), sem((2,)), sem((blocks,)), sem((2,))]
        ),
        compiler_params=pltpu.CompilerParams(vmem_limit_bytes=60 * 1024 * 1024),
    )(own, size, tot, ha, hb, master, momentum)


def solution(mesh):
    finer = Mesh(mesh.devices.reshape(4, 4, 4, 2, 2), AXES)
    replica, shard = AXES[:2], AXES[2:]
    in_specs = (P(replica, shard, None), P(shard, replica), P(shard, replica), P())
    out_specs = (P(shard, replica), P(shard, replica), P(None, replica))
    return jax.shard_map(
        on_device, mesh=finer, in_specs=in_specs, out_specs=out_specs, check_vma=False
    )
```

time: 124 us -> 107 us (0.86)
  Pallas kernels: 123 us -> 105 us
    pallas_call x1 -> x2, Pallas kernels: 115 us -> 95.7 us  [the longest x1 94 us: comm(): return lambda o, d, m, v: call(o, d, m, v)]
where the time goes in v2:
time: 107 us
  Pallas kernels  105 us (98%)
  between operations  1.37 us (1%)
    pallas_call x1, Pallas kernels, comm(): return lambda o, d, m, v: call(o, d, m, v)  94 us
    pallas_call x1, Pallas kernels, on_device(): pl.pallas_call(finish_kernel, name='finish', out_shape=(jax.ShapeDtypeStr...  9.59 us

profile of v2, /device:TPU:1, one launch (start us, length us, event | category | flops | bytes accessed | tf_op | source)
XLA Modules:
  0.0 106.9 jit_solution(15739927431622824265)
XLA Ops:
  0.6 1.6 %size.1 = s32[1]{0:T(128)} custom-call(s32[32]{0:T(128)} %bitcast.33), custom_call_target="tpu_custom_call" | custom-call | tf_op jit(solution)/shard_map/size/pallas_call | solution.py:535
  2.8 94.3 %conditional.1 = (f32[1,128]{1,0:T(1,128)S(1)}, bf16[128,64,512]{2,1,0:T(8,128)(2,1)}, bf16[128,64,512]{2,1,0:T(8,128)(2,1)}) conditional(s32[]{:T(128)} %bitcast.9, (s32[32]{0:T(128)}, bf16[16,32,8192]{2,1,0:T(8,128)(2,1)}, f32[16,32,512]{2,1,0:T(8,128)}, f32[16,32,512]{2,1,0:T(8,128)}) %tuple.48, (s32[32]{0:T(128)}, ...), branch_computations={%region_0.0_spmd, %region_1.0_spmd, %region_2.0_spmd, %region_3.0_... | conditional | bytes 24 | solution.py:552
  2.8 94.0 %reduce_gather_6.1 = (bf16[4,2,2,512,512]{4,3,2,1,0:T(8,128)(2,1)}, bf16[4,2,2,512,512]{4,3,2,1,0:T(8,128)(2,1)}, f32[1,128]{1,0:T(1,128)S(1)}) custom-call(s32[32]{0:T(128)} %get-tuple-element.53.own, bf16[16,32,8192]{2,1,0:T(8,128)(2,1)} %get-tuple-element.54.delta, f32[16,32,512]{2,1,0:T(8,128)} %get-tuple-element.55.master, ...), custom_call_target="tpu_custom_call" | custom-call | tf_op jit(solution)/shard_map/cond/branch_1_fun/reduce_gather_6/pallas_call | solution.py:533
  97.1 9.6 %finish.1 = (f32[512,512]{1,0:T(8,128)}, f32[512,512]{1,0:T(8,128)}, bf16[4096,512]{1,0:T(8,128)(2,1)}) custom-call(s32[32]{0:T(128)} %bitcast.38, s32[1]{0:T(128)} %size.1, f32[1,128]{1,0:T(1,128)S(1)} %get-tuple-element.80.tot, bf16[128,64,512]{2,1,0:T(8,128)(2,1)} %get-tuple-element.81.ha, bf16[128,64,512]{2,1,0:T(8,128)(2,1)} %get-tuple-element.82.hb, ...), custom_call_target="tpu_custom_call" | custom-call | tf_op jit(solution)/shard_map/finish/pallas_call | solution.py:557

commit v3 on v2

v3 whole, which is shorter than its diff:
```python
import functools

import jax
import jax.numpy as jnp
from jax import lax
from jax.experimental import pallas as pl
from jax.experimental.pallas import tpu as pltpu
from jax.sharding import Mesh
from jax.sharding import PartitionSpec as P

BLOCK_ROWS = 128
SLOTS = 4
HALF_BLOCK = 64
AXES = ("zh", "x", "y", "zl", "core")
MESH = pl.DeviceIdType.MESH
R = 32
DIRECT = 1
F32 = jnp.float32
BF16 = jnp.bfloat16


def comm_kernel(
    nc,
    own, delta, master, momentum,
    ha, hb, tot,
    d, xt, xr, xe, zr, ze, zf, mst, mom, axs, axr, acc, n1, n2,
    load_sem, ex_sem, mm_sem, xt_sem, ax_sem,
    xrr, xer, zrr, zer, zf_sem, send_sem,
    gr0, gr1, gr2, gr3, gs, n_sem,
):
    chunks = d.shape[0]
    extra = chunks - nc
    per_block = BLOCK_ROWS // R
    half = R // 2
    cols = master.shape[2]
    zh, x, y = lax.axis_index("zh"), lax.axis_index("x"), lax.axis_index("y")
    zl, core = lax.axis_index("zl"), lax.axis_index("core")
    halves = (pl.ds(0, half), pl.ds(half, half))
    replica = zh * 4 + x
    shard = (y * 2 + zl) * 2 + core
    twin = (y * 2 + zl) * 2 + 1 - core

    def ring(i):
        return lax.rem(i + 1, 4), lax.rem(i + 3, 4), lax.rem(i + 2, 4)

    def lanes(i):
        return pl.ds(pl.multiple_of(i * cols, cols), cols)

    xn, zn, yn = ring(x), ring(zh), ring(y)
    yp, ym, yo = yn
    zl2, core2 = 1 - zl, 1 - core

    barrier = pltpu.get_barrier_semaphore()
    for peer in (
        {"x": xn[0]}, {"x": xn[1]}, {"zh": zn[0]}, {"zh": zn[1]},
        {"y": yp}, {"y": ym}, {"zl": zl2}, {"core": core2},
    ):
        pl.semaphore_signal(barrier, inc=1, device_id=peer, device_id_type=MESH)

    def load(c):
        for k in range(4):
            pltpu.make_async_copy(
                delta.at[c, :, pl.ds(k * 4 * cols, 4 * cols)], d.at[c, k], load_sem.at[c]
            ).start()

    load(0)
    load(1)
    get_m = pltpu.make_async_copy(master, mst, mm_sem.at[0])
    get_v = pltpu.make_async_copy(momentum, mom, mm_sem.at[1])
    get_m.start()
    get_v.start()
    if extra:
        for k in range(4):
            pltpu.make_async_copy(
                delta.at[pl.ds(nc, extra), :, pl.ds(k * 4 * cols, 4 * cols)],
                d.at[pl.ds(nc, extra), k], ex_sem,
            ).start()

    def load_next(c, carry):
        load(c)
        return carry

    lax.fori_loop(2, nc, load_next, 0)

    count, twin_count = jnp.int32(0), jnp.int32(0)
    for b in range(own.shape[0]):
        count = count + (own[b] == shard).astype(jnp.int32)
        twin_count = twin_count + (own[b] == twin).astype(jnp.int32)

    def spare(c):
        i = c - per_block * count
        return i, (i >= 0) & (i < extra), jnp.clip(i, 0, max(extra - 1, 0))

    def is_live(c):
        i, inside, _ = spare(c)
        live = c < per_block * count
        if extra:
            live = live | (inside & (i + nc < per_block * twin_count))
        return live

    acc[...] = jnp.zeros_like(acc)
    pl.semaphore_wait(barrier, 8)

    def send(src, dst, ss, rs, peer):
        return pltpu.make_async_remote_copy(
            src_ref=src, dst_ref=dst, send_sem=ss, recv_sem=rs, device_id=peer, device_id_type=MESH
        )

    def xt_copy():
        return send(d.at[pl.ds(nc, extra)], xt, xt_sem.at[0], xt_sem.at[1], {"core": core2})

    def ax_copy():
        return send(axs, axr, ax_sem.at[0], ax_sem.at[1], {"core": core2})

    def wait_for(ref, sem):
        pltpu.make_async_copy(ref, ref, sem).wait()

    class Phase:
        def __init__(self, axis, near, slab, r, e, rr, er, first):
            self.axis, self.near, self.slab = axis, near, slab
            self.r, self.e, self.rr, self.er, self.first = r, e, rr, er, first

        def relay(self, c, h):
            return send(
                self.slab(c, self.near[2], h), self.r.at[c, h],
                send_sem.at[self.first], self.rr.at[c], {self.axis: self.near[h]},
            )

        def direct(self, c, h):
            return send(
                self.slab(c, self.near[h], 1 - h), self.e.at[c, 0, h],
                send_sem.at[self.first + 1], self.er.at[c], {self.axis: self.near[h]},
            )

        def summed(self, c, h):
            return send(
                self.slab(c, self.near[h], h), self.e.at[c, 1, h],
                send_sem.at[self.first + 2], self.er.at[c], {self.axis: self.near[h]},
            )

        def wait_relay(self, c):
            wait_for(self.r.at[c], self.rr.at[c])

        def wait_sends(self):
            for i, ref in enumerate((self.r, self.e.at[:, 0], self.e.at[:, 1])):
                wait_for(ref, send_sem.at[self.first + i])

    xph = Phase("x", xn, lambda c, i, h: d.at[c, :, halves[h], lanes(i)], xr, xe, xrr, xer, 0)
    zph = Phase("zh", zn, lambda c, i, h: d.at[c, i, halves[h], lanes(x)], zr, ze, zrr, zer, 3)

    def start_x(c, fixed=False):
        pltpu.make_async_copy(d.at[c], d.at[c], load_sem.at[c]).wait()
        if extra and not fixed:
            _, use, at = spare(c)

            @pl.when(c == per_block)
            def _():
                xt_copy().wait_recv()

            @pl.when(c >= per_block)
            def _():
                for k in range(4):
                    d[c, k] = jnp.where(use, xt[at, k], d[c, k])
        for h in range(2):
            xph.relay(c, h).start()
        for h in range(2):
            xph.direct(c, h).start()

    def sum_x(c):
        xph.wait_relay(c)
        for h in range(2):
            for k in range(4):
                to = lanes(xn[h])
                d[c, k, halves[h], to] = (
                    d[c, k, halves[h], to].astype(F32) + xr[c, h, k].astype(F32)
                ).astype(BF16)
            xph.summed(c, h).start()

    def z_full(k, j):
        return send(
            d.at[nc - DIRECT + k, zn[j], :, lanes(x)], zf.at[k, j],
            zf_sem.at[0], zf_sem.at[1 + k], {"zh": zn[j]},
        )

    def end_x(c, final=None):
        wait_for(xe.at[c], xer.at[c])
        for h in range(2):
            for k in range(4):
                d[c, k, halves[h], lanes(x)] = (
                    d[c, k, halves[h], lanes(x)].astype(F32)
                    + xe[c, 1, h, k].astype(F32)
                    + xe[c, 0, 1 - h, k].astype(F32)
                ).astype(BF16)
        if final is not None:
            for j in (2, 0, 1):
                z_full(final, j).start()
            return
        for h in range(2):
            zph.relay(c, h).start()
        for h in range(2):
            zph.direct(c, h).start()

    def sum_z(c):
        zph.wait_relay(c)
        for h in range(2):
            to = zn[h]
            d[c, to, halves[h], lanes(x)] = (
                d[c, to, halves[h], lanes(x)].astype(F32) + zr[c, h].astype(F32)
            ).astype(BF16)
            zph.summed(c, h).start()

    def g_copy(k, c, i):
        g = (ha, hb)[k]
        mine_at, other_at = g.at[y, zl, core, c], g.at[y, zl2, core, c]
        up, down = g.at[ym, :, core, c, halves[0], :], g.at[yp, :, core, c, halves[1], :]
        ref = (mine_at, mine_at, mine_at, other_at, other_at, up, down, g.at[:, :, core, c])[i]
        peer = (
            {"zl": zl2}, {"y": yp}, {"y": ym}, {"y": yp}, {"y": ym}, {"y": yp}, {"y": ym}, {"core": core2},
        )[i]
        arrive = (gr0, gr1, gr1, gr1, gr1, gr2, gr2)[i].at[k, c] if i < 7 else gr3.at[k]
        return send(ref, ref, gs.at[k, i], arrive, peer)

    def g_start(k, c):
        for i in (0, 1, 2):
            g_copy(k, c, i).start()

    def g_second(k, c):
        g_copy(k, c, 0).wait_recv()
        for i in (3, 4):
            g_copy(k, c, i).start()

    def g_third(k, c):
        wait_for((ha, hb)[k].at[0, 0, 0, pl.ds(0, 4)], gr1.at[k, c])
        for i in (5, 6):
            g_copy(k, c, i).start()

    def g_last(k, c):
        wait_for((ha, hb)[k].at[0, 0, 0, pl.ds(0, 2)], gr2.at[k, c])
        g_copy(k, c, 7).start()

    def g_drain(k):
        g = (ha, hb)[k]
        for i in range(7):
            wait_for(g.at[0, 0, 0, pl.ds(0, nc)], gs.at[k, i])
        for arrive in (gs.at[k, 7], gr3.at[k]):
            wait_for(g.at[:, :, 0, pl.ds(0, nc)], arrive)

    def end_z(c, final=None):
        if final is not None:
            wait_for(zf.at[final], zf_sem.at[1 + final])
        else:
            wait_for(ze.at[c], zer.at[c])
        live = is_live(c)
        for h in range(2):
            value = d[c, zh, halves[h], lanes(x)].astype(F32)
            if final is not None:
                parts = [zf[final, j, halves[h], :] for j in range(3)]
            else:
                parts = [ze[c, 1, h], ze[c, 0, 1 - h]]
            for part in parts:
                value = value + part.astype(F32)
            value = value * F32(0.0625)
            value = jnp.where(live, value, F32(0.0))
            hb[y, zl, core, c, halves[h], :] = value.astype(BF16)
            square = jnp.sum((value * value).reshape(half // 8, 8, cols), axis=0)
            part = square[:, :128]
            for k in range(1, cols // 128):
                part = part + square[:, k * 128:(k + 1) * 128]
            acc[...] += part
        g_start(1, c)

    def a_of(c, r):
        return (mst[c, r, :] - F32(0.567) * mom[c, r, :]).astype(BF16)

    def start_a(c, fixed=False):
        if extra and not fixed:

            @pl.when(c == per_block)
            def _():
                ax_copy().wait_recv()

        for r in halves:
            ha[y, zl, core, c, r, :] = a_of(c, r)
        if extra and not fixed:
            _, use, spot = spare(c)

            @pl.when(c >= per_block)
            def _():
                for r in halves:
                    value = ha[y, zl, core, c, r, :]
                    ha[y, zl, core, c, r, :] = jnp.where(use, axr[spot, r, :], value)
        g_start(0, c)

    def at(t, lag, f):
        @pl.when((t >= lag) & (t < nc + lag))
        def _():
            f(t - lag)

    def pair(t, lag, f):
        @pl.when((t >= lag) & (t < nc // 2 + lag))
        def _():
            f(2 * (t - lag))
            f(2 * (t - lag) + 1)

    second = [functools.partial(g_second, k) for k in range(2)]
    third = [functools.partial(g_third, k) for k in range(2)]
    last = [functools.partial(g_last, k) for k in range(2)]

    def loop_body(t, carry):
        @pl.when((t >= 1) & (t < nc - 1))
        def _():
            start_x(t + 1)

        pair(t, -1, start_a)
        at(t, 0, sum_x)
        pair(t, 0, second[0])
        at(t, 1, end_x)
        pair(t, 1, third[0])
        at(t, 2, sum_z)
        at(t, 3, end_z)
        pair(t, 2, last[0])
        at(t, 4, second[1])
        at(t, 5, third[1])
        at(t, 6, last[1])
        return carry

    def direct(c):
        return c - (nc - DIRECT) if c >= nc - DIRECT else None

    def norm1(i):
        q = lax.rem(replica + i, 16)
        return send(
            n1.at[replica], n1.at[replica], n_sem.at[0], n_sem.at[1],
            {"zh": q // 4, "x": lax.rem(q, 4)},
        )

    def norm2(i):
        q = lax.rem(shard + i, 16)
        return send(
            n2.at[shard], n2.at[shard], n_sem.at[2], n_sem.at[3],
            {"y": q // 4, "zl": lax.rem(q // 2, 2), "core": lax.rem(q, 2)},
        )

    start_x(0, fixed=True)
    start_x(1, fixed=True)
    get_m.wait()
    get_v.wait()
    start_a(0, fixed=True)
    start_a(1, fixed=True)
    if extra:
        wait_for(d.at[pl.ds(nc, extra)], ex_sem)
        xt_copy().start()
        for e in range(extra):
            axs[e] = a_of(nc + e, slice(None))
        ax_copy().start()
    lax.fori_loop(0, nc - 1, loop_body, 0)

    n = nc
    sum_x(n - 1)
    end_x(n - 2, final=direct(n - 2))
    sum_z(n - 3)
    end_z(n - 4)
    second[1](n - 5)
    third[1](n - 6)
    last[1](n - 7)
    end_x(n - 1, final=direct(n - 1))
    if direct(n - 2) is None:
        sum_z(n - 2)
    second[1](n - 4)
    end_z(n - 3)
    if direct(n - 1) is None:
        sum_z(n - 1)
    third[1](n - 5)
    last[1](n - 6)
    end_z(n - 2, final=direct(n - 2))
    end_z(n - 1, final=direct(n - 1))
    n1[replica] = jnp.sum(acc[...], axis=0, keepdims=True)
    for i in range(1, 16):
        norm1(i).start()
    second[1](n - 3)
    third[1](n - 4)
    second[1](n - 2)
    last[1](n - 5)
    second[1](n - 1)
    third[1](n - 3)
    last[1](n - 4)
    third[1](n - 2)
    xph.wait_sends()
    zph.wait_sends()
    if extra:
        xt_copy().wait_send()
        ax_copy().wait_send()
    last[1](n - 3)
    third[1](n - 1)
    some = pl.ds(0, 15)
    wait_for(n1.at[some], n_sem.at[1])
    n2[shard] = jnp.sum(n1[...], axis=0)
    for i in range(1, 16):
        norm2(i).start()
    last[1](n - 2)
    last[1](n - 1)
    g_drain(0)
    if DIRECT:
        wait_for(zf, zf_sem.at[0])
    wait_for(n1.at[some], n_sem.at[0])
    wait_for(n2.at[some], n_sem.at[3])
    tot[...] = jnp.sum(n2[...], axis=0)
    wait_for(n2.at[some], n_sem.at[2])
    g_drain(1)


def finish_kernel(
    own, size, tot, ha, hb, master, momentum,
    master_out, momentum_out, params,
    p, m, v, mo, vo, counts, slots, in_sem, out_sem,
):
    blocks = own.shape[0]
    per = params.shape[0] // blocks // HALF_BLOCK
    limit_of = SLOTS * per
    shard = (lax.axis_index("y") * 2 + lax.axis_index("zl")) * 2 + lax.axis_index("core")
    n = size[0]
    get_m = pltpu.make_async_copy(master, m, in_sem.at[0])
    get_v = pltpu.make_async_copy(momentum, v, in_sem.at[1])
    get_m.start()
    get_v.start()
    for k in range(16):
        counts[k] = 0
        slots[k] = 0
    for i in range(blocks):
        counts[own[i]] = counts[own[i]] + 1

    def flat(k, q):
        other = k + 1 - 2 * lax.rem(k, 2)
        return jnp.where(q < n, k * limit_of + q, other * limit_of + q - n + per * counts[other])

    limit = 0.5 * jnp.sqrt(jnp.full((1, 1), params.shape[0] * params.shape[1] * 16, F32))
    total = jnp.sum(tot[...], axis=1, keepdims=True)
    factor = jnp.minimum(F32(1.0), limit / (jnp.sqrt(total) + F32(1e-06)))
    scale = F32(1.33) * factor

    def block(i, carry):
        k = own[i]
        j = slots[k]
        slots[k] = j + 1
        for r in range(per):
            f = flat(k, j * per + r)
            for h in range(2):
                w = pl.ds(h * 32, 32)
                p[i, pl.ds(r * HALF_BLOCK + h * 32, 32), :] = (
                    ha[f, w, :].astype(F32) - scale * hb[f, w, :].astype(F32)
                ).astype(BF16)
        rows = pl.ds(pl.multiple_of(i * BLOCK_ROWS, BLOCK_ROWS), BLOCK_ROWS)
        pltpu.make_async_copy(p.at[i], params.at[rows], out_sem.at[2]).start()
        return carry

    lax.fori_loop(0, 8, block, 0)
    get_m.wait()
    get_v.wait()
    count = counts[shard]

    def update(q, carry):
        live = q < per * count
        f = jnp.where(live, flat(shard, q), 0)
        for h in range(2):
            r = pl.ds(pl.multiple_of(q * HALF_BLOCK + h * 32, 32), 32)
            grad = factor * hb[f, pl.ds(h * 32, 32), :].astype(F32)
            old = v[r, :]
            new = jnp.where(live, F32(0.9) * old + grad, old)
            z = m[r, :]
            vo[r, :] = new
            mo[r, :] = jnp.where(live, z - F32(0.7) * (grad + F32(0.9) * new), z)
        return carry

    lax.fori_loop(0, limit_of, update, 0)
    put_m = pltpu.make_async_copy(mo, master_out, out_sem.at[0])
    put_v = pltpu.make_async_copy(vo, momentum_out, out_sem.at[1])
    put_m.start()
    put_v.start()
    lax.fori_loop(8, blocks, block, 0)
    put_m.wait()
    put_v.wait()
    pltpu.make_async_copy(p, p, out_sem.at[2]).wait()


def size_kernel(own, size):
    chips = [jnp.int32(0)] * 8
    for i in range(own.shape[0]):
        chip = own[i] // 2
        chips = [n + (chip == k).astype(jnp.int32) for k, n in enumerate(chips)]
    most = functools.reduce(jnp.maximum, chips)
    size[0] = jnp.maximum(most, SIZES[0])


SIZES = (5, 6, 7, 8)


def on_device(deltas, master, momentum, block_owner):
    rows, cols = master.shape
    width = deltas.shape[2]
    chunks = rows // R
    half = R // 2
    own = block_owner.reshape(-1)
    blocks = own.shape[0]
    any_spec = pl.BlockSpec(memory_space=pl.ANY)
    vmem = pl.BlockSpec(memory_space=pltpu.VMEM)
    smem = pl.BlockSpec(memory_space=pltpu.SMEM)
    sem = pltpu.SemaphoreType.DMA
    gathered = jax.ShapeDtypeStruct((4, 2, 2, chunks, R, cols), BF16)

    def comm(size, ident):
        nc = size * HALF_BLOCK // R
        extra = max(chunks - nc, 1)
        call = pl.pallas_call(
            functools.partial(comm_kernel, nc),
            name=f"reduce_gather_{size}",
            out_shape=(gathered, gathered, jax.ShapeDtypeStruct((1, 128), F32)),
            in_specs=[smem, any_spec, any_spec, any_spec],
            out_specs=(vmem, vmem, vmem),
            scratch_shapes=(
                [pltpu.VMEM((chunks, 4, R, 4 * cols), BF16)]
                + [pltpu.VMEM((extra, 4, R, 4 * cols), BF16)]
                + [pltpu.VMEM((nc, 2, 4, half, cols), BF16)]
                + [pltpu.VMEM((nc, 2, 2, 4, half, cols), BF16)]
                + [pltpu.VMEM((nc - DIRECT, 2, half, cols), BF16)]
                + [pltpu.VMEM((nc - DIRECT, 2, 2, half, cols), BF16)]
                + [pltpu.VMEM((max(DIRECT, 1), 3, R, cols), BF16)]
                + [pltpu.VMEM((chunks, R, cols), F32)] * 2
                + [pltpu.VMEM((extra, R, cols), BF16)] * 2
                + [pltpu.VMEM((8, 128), F32)]
                + [pltpu.VMEM((16, 1, 128), F32)] * 2
                + [sem((nc,)), sem, sem((2,)), sem((2,)), sem((2,))]
                + [sem((nc,))] * 2
                + [sem((nc - DIRECT,))] * 2
                + [sem((1 + DIRECT,)), sem((6,))]
                + [sem((2, nc))] * 3
                + [sem((2,)), sem((2, 8)), sem((4,))]
            ),
            compiler_params=pltpu.CompilerParams(
                collective_id=ident, has_side_effects=True, vmem_limit_bytes=30 * 1024 * 1024
            ),
        )
        return lambda o, d, m, v: call(o, d, m, v)

    size = pl.pallas_call(
        size_kernel,
        name="size",
        out_shape=jax.ShapeDtypeStruct((1,), jnp.int32),
        in_specs=[smem],
        out_specs=smem,
    )(own)
    operands = (
        own,
        deltas.reshape(chunks, R, width),
        master.reshape(chunks, R, cols),
        momentum.reshape(chunks, R, cols),
    )
    branches = [comm(s, i) for i, s in enumerate(SIZES)]
    if len(branches) == 1:
        ha, hb, tot = branches[0](*operands)
    else:
        ha, hb, tot = lax.switch(size[0] - SIZES[0], branches, *operands)
    parts = 16 * rows // HALF_BLOCK
    ha = ha.reshape(parts, HALF_BLOCK, cols)
    hb = hb.reshape(parts, HALF_BLOCK, cols)
    return pl.pallas_call(
        finish_kernel,
        name="finish",
        out_shape=(
            jax.ShapeDtypeStruct((rows, cols), F32),
            jax.ShapeDtypeStruct((rows, cols), F32),
            jax.ShapeDtypeStruct((blocks * BLOCK_ROWS, cols), BF16),
        ),
        in_specs=[smem, smem, vmem, vmem, vmem] + [any_spec] * 2,
        out_specs=(any_spec, any_spec, any_spec),
        scratch_shapes=(
            [pltpu.VMEM((blocks, BLOCK_ROWS, cols), BF16)]
            + [pltpu.VMEM((rows, cols), F32)] * 4
            + [pltpu.SMEM((16,), jnp.int32)] * 2
            + [sem((2,)), sem((3,))]
        ),
        compiler_params=pltpu.CompilerParams(vmem_limit_bytes=12 * 1024 * 1024),
    )(own, size, tot, ha, hb, master, momentum)


def solution(mesh):
    finer = Mesh(mesh.devices.reshape(4, 4, 4, 2, 2), AXES)
    replica, shard = AXES[:2], AXES[2:]
    in_specs = (P(replica, shard, None), P(shard, replica), P(shard, replica), P())
    out_specs = (P(shard, replica), P(shard, replica), P(None, replica))
    return jax.shard_map(
        on_device, mesh=finer, in_specs=in_specs, out_specs=out_specs, check_vma=False
    )
```

time: 107 us -> 95.1 us (0.89)
  Pallas kernels: 105 us -> 93.6 us
    pallas_call x1, Pallas kernels: 94 us -> 85.9 us  [comm(): return lambda o, d, m, v: call(o, d, m, v)]
    pallas_call x1, Pallas kernels: 9.59 us -> 6.1 us  [on_device(): pl.pallas_call(finish_kernel, name='finish', out_shape=(jax.ShapeDtypeStr...]
where the time goes in v3:
time: 95.1 us; the launch traced here: 95 us
  Pallas kernels  93.6 us (98%)
  between operations  1.33 us (1%)
    pallas_call x1, Pallas kernels, comm(): return lambda o, d, m, v: call(o, d, m, v)  85.9 us
    pallas_call x1, Pallas kernels, on_device(): pl.pallas_call(finish_kernel, name='finish', out_shape=(jax.ShapeDtypeStr...  6.1 us

profile of v3, /device:TPU:1, one launch (start us, length us, event | category | flops | bytes accessed | tf_op | source)
XLA Modules:
  0.0 95.0 jit_solution(11102034818481487971)
XLA Ops:
  0.6 1.6 %size.1 = s32[1]{0:T(128)} custom-call(s32[32]{0:T(128)} %bitcast.33), custom_call_target="tpu_custom_call" | custom-call | tf_op jit(solution)/shard_map/size/pallas_call | solution.py:544
  3.0 85.9 %conditional.1 = (f32[1,128]{1,0:T(1,128)S(1)}, bf16[128,64,512]{2,1,0:T(8,128)(2,1)S(1)}, bf16[128,64,512]{2,1,0:T(8,128)(2,1)S(1)}) conditional(s32[]{:T(128)} %bitcast.9, (s32[32]{0:T(128)}, bf16[16,32,8192]{2,1,0:T(8,128)(2,1)}, f32[16,32,512]{2,1,0:T(8,128)}, f32[16,32,512]{2,1,0:T(8,128)}) %tuple.48, ...), branch_computations={%region_0.0_spmd, %region_1.0_spmd, %region_2.0_spmd, %region_3.0_... | conditional | bytes 24 | solution.py:561
  3.0 85.9 %reduce_gather_6.1 = (bf16[4,2,2,16,32,512]{5,4,3,2,1,0:T(8,128)(2,1)S(1)}, bf16[4,2,2,16,32,512]{5,4,3,2,1,0:T(8,128)(2,1)S(1)}, f32[1,128]{1,0:T(1,128)S(1)}) custom-call(s32[32]{0:T(128)} %get-tuple-element.53.own, bf16[16,32,8192]{2,1,0:T(8,128)(2,1)} %get-tuple-element.54.delta, f32[16,32,512]{2,1,0:T(8,128)} %get-tuple-element.55.master, ...), custom_call_target="tpu_custom_call" | custom-call | tf_op jit(solution)/shard_map/cond/branch_1_fun/reduce_gather_6/pallas_call | solution.py:542
  88.9 6.1 %finish.1 = (f32[512,512]{1,0:T(8,128)}, f32[512,512]{1,0:T(8,128)}, bf16[4096,512]{1,0:T(8,128)(2,1)}) custom-call(s32[32]{0:T(128)} %bitcast.38, s32[1]{0:T(128)} %size.1, f32[1,128]{1,0:T(1,128)S(1)} %get-tuple-element.80.tot, bf16[128,64,512]{2,1,0:T(8,128)(2,1)S(1)} %get-tuple-element.81.ha, bf16[128,64,512]{2,1,0:T(8,128)(2,1)S(1)} %get-tuple-element.82.hb, ...), custom_call_target="tpu_custom_call" | custom-call | tf_op jit(solution)/shard_map/finish/pallas_call | solution.py:565
